TPU v7x, 16 devices: a whole 2x2x2 slice. The times are simulated.
16 devices in a mesh: data: 16 (over z, y, x, core).
Axes of the slice: x: 2, y: 2, z: 2, core: 2. Of those that a mesh axis runs over, the one named last changes fastest.
Arguments:
- tokens: bfloat16 [65536, 768], P('data')
- targets: bfloat16 [65536, 768], P('data')
- w_in: bfloat16 [4, 768, 3072], replicated
- w_out: bfloat16 [4, 3072, 768], replicated
Outputs:
- output 1: float32 [4, 768, 3072], replicated
- output 2: float32 [4, 3072, 768], replicated
All inputs are finite; a program needn't handle non-finite values.
Results may differ from a plain program's by a relative error of at most 0.0147433.
Values are sent between devices in bfloat16 or wider.
A program may use at most 1 GiB of HBM per device.

v0:
```python
import math
import jax
import jax.numpy as jnp
from jax import lax
from jax.sharding import PartitionSpec as P

CONTRACT_ROWS = (((0,), (0,)), ((), ()))
CONTRACT_COLS = (((1,), (1,)), ((), ()))


def solution(mesh):
    axis_name = mesh.axis_names[0]

    def grad_program(tokens, targets, w_in, w_out):
        total_tokens, model_width = tokens.shape
        target_scale = 1.0 + 16.0 * math.sqrt(total_tokens / model_width)
        loss_coef = 1.0 / (target_scale * math.sqrt(total_tokens))
        layers = w_in.shape[0]

        def device_step(tok_rows, tgt_rows, w_first_all, w_second_all):
            hidden = tok_rows
            saved_fwd = []
            for layer_idx in range(layers):
                pre_act = jnp.dot(hidden, w_first_all[layer_idx], preferred_element_type=jnp.float32).astype(jnp.bfloat16)
                activ_f32, gelu_back = jax.vjp(jax.nn.gelu, pre_act.astype(jnp.float32))
                activ = activ_f32.astype(jnp.bfloat16)
                saved_fwd.append((hidden, activ, gelu_back))
                branch = jnp.dot(activ, w_second_all[layer_idx], preferred_element_type=jnp.float32)
                hidden = (hidden.astype(jnp.float32) + branch).astype(jnp.bfloat16)
            error_rows = hidden.astype(jnp.float32) - tgt_rows.astype(jnp.float32)
            grad_h = (error_rows * loss_coef).astype(jnp.bfloat16)
            summed_in = []
            summed_out = []
            for layer_idx in reversed(range(layers)):
                layer_in, activ, gelu_back = saved_fwd[layer_idx]
                local_out = lax.dot_general(activ, grad_h, CONTRACT_ROWS, preferred_element_type=jnp.float32).astype(jnp.bfloat16)
                grad_act = lax.dot_general(grad_h, w_second_all[layer_idx], CONTRACT_COLS, preferred_element_type=jnp.float32).astype(jnp.bfloat16)
                grad_pre = gelu_back(grad_act.astype(jnp.float32))[0].astype(jnp.bfloat16)
                local_in = lax.dot_general(layer_in, grad_pre, CONTRACT_ROWS, preferred_element_type=jnp.float32).astype(jnp.bfloat16)
                if layer_idx > 0:
                    grad_back = lax.dot_general(grad_pre, w_first_all[layer_idx], CONTRACT_COLS, preferred_element_type=jnp.float32).astype(jnp.bfloat16)
                    grad_h = grad_h + grad_back
                layer_in_sum, layer_out_sum = lax.psum((local_in.astype(jnp.float32), local_out.astype(jnp.float32)), axis_name)
                summed_in.append(layer_in_sum)
                summed_out.append(layer_out_sum)
            return jnp.stack(summed_in[::-1]), jnp.stack(summed_out[::-1])

        return jax.shard_map(device_step, mesh=mesh, in_specs=(P(axis_name), P(axis_name), P(), P()), out_specs=(P(), P()), check_vma=False)(tokens, targets, w_in, w_out)

    return grad_program
```

profile of v0, /device:TPU:0, one launch (start us, length us, event | category | flops | bytes accessed | tf_op | source)
XLA Modules:
  0.0 1560.5 jit_solution(4307837414338179820)
XLA Ops:
  7.2 0.0 all-reduce.3.cloned.1.call-start
  7.2 0.0 copy-start
  7.2 27.0 %convolution_convert_fusion.3 = bf16[4096,3072]{1,0:T(8,128)(2,1)} fusion(bf16[4096,768]{1,0:T(8,128)(2,1)} %param.4, bf16[4,768,3072]{2,1,0:T(8,128)(2,1)} %param.6), kind=kOutput, calls=%fused_computation.74 | convolution fusion | flops 19339935744 | bytes 36175872 | tf_op jit(solution)/shard_map/dot_general | solution.py:24
  34.2 0.0 copy-done
  34.2 36.6 %add_convert_fusion.3 = bf16[4096,768]{1,0:T(8,128)(2,1)} fusion(bf16[4096,768]{1,0:T(8,128)(2,1)S(1)} %copy-done, bf16[4,3072,768]{2,1,0:T(8,128)(2,1)} %param.7, bf16[4096,3072]{1,0:T(8,128)(2,1)} %convolution_convert_fusion.3), kind=kOutput, calls=%fused_computation.80 | convolution fusion | flops 19462619136 | bytes 42467328 | tf_op jit(solution)/shard_map/dot_general | solution.py:28
  70.8 0.0 copy-start.1
  70.8 27.8 %convolution_convert_fusion.2 = bf16[4096,3072]{1,0:T(8,128)(2,1)} fusion(bf16[4096,768]{1,0:T(8,128)(2,1)} %add_convert_fusion.3, bf16[4,768,3072]{2,1,0:T(8,128)(2,1)} %param.6), kind=kOutput, calls=%fused_computation.73 | convolution fusion | flops 19339935744 | bytes 36175872 | tf_op jit(solution)/shard_map/dot_general | solution.py:24
  98.6 0.0 copy-done.1
  98.6 36.4 %add_convert_fusion.2 = bf16[4096,768]{1,0:T(8,128)(2,1)} fusion(bf16[4096,768]{1,0:T(8,128)(2,1)S(1)} %copy-done.1, bf16[4,3072,768]{2,1,0:T(8,128)(2,1)} %param.7, bf16[4096,3072]{1,0:T(8,128)(2,1)} %convolution_convert_fusion.2), kind=kOutput, calls=%fused_computation.79 | convolution fusion | flops 19462619136 | bytes 42467328 | tf_op jit(solution)/shard_map/dot_general | solution.py:28
  135.0 0.0 slice-start
  135.0 27.1 %convolution_convert_fusion.1 = bf16[4096,3072]{1,0:T(8,128)(2,1)} fusion(bf16[4096,768]{1,0:T(8,128)(2,1)} %add_convert_fusion.2, bf16[4,768,3072]{2,1,0:T(8,128)(2,1)} %param.6), kind=kOutput, calls=%fused_computation.72 | convolution fusion | flops 19339935744 | bytes 36175872 | tf_op jit(solution)/shard_map/dot_general | solution.py:24
  162.1 0.0 slice-start.1
  162.1 37.1 %add_convert_fusion.1 = bf16[4096,768]{1,0:T(8,128)(2,1)} fusion(bf16[4096,768]{1,0:T(8,128)(2,1)} %add_convert_fusion.2, bf16[4,3072,768]{2,1,0:T(8,128)(2,1)} %param.7, bf16[4096,3072]{1,0:T(8,128)(2,1)} %convolution_convert_fusion.1), kind=kOutput, calls=%fused_computation.78 | convolution fusion | flops 19462619136 | bytes 42467328 | tf_op jit(solution)/shard_map/dot_general | solution.py:28
  199.2 27.0 %convolution_convert_fusion = bf16[4096,3072]{1,0:T(8,128)(2,1)} fusion(bf16[4096,768]{1,0:T(8,128)(2,1)} %add_convert_fusion.1, bf16[4,768,3072]{2,1,0:T(8,128)(2,1)} %param.6), kind=kOutput, calls=%fused_computation.71 | convolution fusion | flops 19339935744 | bytes 36175872 | tf_op jit(solution)/shard_map/dot_general | solution.py:24
  226.2 0.0 slice-done
  226.2 0.0 slice-done.1
  226.3 36.8 %multiply_convert_fusion = bf16[4096,768]{1,0:T(8,128)(2,1)S(1)} fusion(bf16[4096,768]{1,0:T(8,128)(2,1)S(1)} %bitcast.105, bf16[4096,768]{1,0:T(8,128)(2,1)} %add_convert_fusion.1, bf16[4,3072,768]{2,1,0:T(8,128)(2,1)} %param.7, bf16[4096,3072]{1,0:T(8,128)(2,1)} %convolution_convert_fusion), kind=kOutput, calls=%fused_computation.76 | convolution fusion | flops 19478347776 | bytes 48758784 | tf_op jit(solution)/shard_map/dot_general | solution.py:28
  263.1 0.0 copy-start.7
  263.1 33.7 %bitcast_convert_fusion = f32[1,3072,768]{2,1,0:T(8,128)} fusion(bf16[4096,768]{1,0:T(8,128)(2,1)S(1)} %multiply_convert_fusion, bf16[4096,3072]{1,0:T(8,128)(2,1)} %convolution_convert_fusion), kind=kOutput, calls=%fused_computation.96 | convolution fusion | flops 19457900544 | bytes 40894464 | tf_op jit(solution)/shard_map/dot_general | solution.py:36
  296.8 0.0 copy-done.7
  296.9 55.9 %fusion.6 = bf16[4096,3072]{1,0:T(8,128)(2,1)} fusion(bf16[4096,3072]{1,0:T(8,128)(2,1)} %convolution_convert_fusion, bf16[4096,768]{1,0:T(8,128)(2,1)S(1)} %multiply_convert_fusion, bf16[4,3072,768]{2,1,0:T(8,128)(2,1)} %param.7), kind=kOutput, calls=%fused_computation.30 | convolution fusion | flops 19616759808 | bytes 61341696 | tf_op jit(solution)/shard_map/dot_general | solution.py:37
  352.7 0.0 copy-start.4
  352.7 27.5 %fusion.48 = bf16[4096,768]{1,0:T(8,128)(2,1)} fusion(bf16[4096,768]{1,0:T(8,128)(2,1)} %copy-done.7, bf16[4096,3072]{1,0:T(8,128)(2,1)} %fusion.6, bf16[4,768,3072]{2,1,0:T(8,128)(2,1)} %param.6), kind=kOutput, calls=%fused_computation.85 | convolution fusion | flops 19333644288 | bytes 42467328 | tf_op jit(solution)/shard_map/dot_general | solution.py:41
  380.2 0.0 copy-done.4
  380.2 0.0 copy-start.5
  380.2 25.4 %bitcast_convert_fusion.4 = f32[1,768,3072]{1,2,0:T(8,128)} fusion(bf16[4096,768]{1,0:T(8,128)(2,1)S(1)} %copy-done.4, bf16[4096,3072]{1,0:T(8,128)(2,1)} %fusion.6), kind=kOutput, calls=%fused_computation.100 | convolution fusion | flops 19332071424 | bytes 40894464 | tf_op jit(solution)/shard_map/dot_general | solution.py:39
  405.7 0.0 copy-done.5
  405.7 32.2 %bitcast_convert_fusion.1 = f32[1,3072,768]{2,1,0:T(8,128)} fusion(bf16[4096,768]{1,0:T(8,128)(2,1)S(1)} %copy-done.5, bf16[4096,3072]{1,0:T(8,128)(2,1)} %convolution_convert_fusion.1), kind=kOutput, calls=%fused_computation.97 | convolution fusion | flops 19457900544 | bytes 40894464 | tf_op jit(solution)/shard_map/dot_general | solution.py:36
  437.8 56.4 %fusion.9 = bf16[4096,3072]{1,0:T(8,128)(2,1)} fusion(bf16[4096,3072]{1,0:T(8,128)(2,1)} %convolution_convert_fusion.1, bf16[4096,768]{1,0:T(8,128)(2,1)S(1)} %copy-done.5, bf16[4,3072,768]{2,1,0:T(8,128)(2,1)} %param.7), kind=kOutput, calls=%fused_computation.33 | convolution fusion | flops 19616759808 | bytes 61341696 | tf_op jit(solution)/shard_map/dot_general | solution.py:37
  494.2 0.0 copy-start.3
  494.2 27.5 %fusion.49 = bf16[4096,768]{1,0:T(8,128)(2,1)} fusion(bf16[4096,768]{1,0:T(8,128)(2,1)} %fusion.48, bf16[4096,3072]{1,0:T(8,128)(2,1)} %fusion.9, bf16[4,768,3072]{2,1,0:T(8,128)(2,1)} %param.6), kind=kOutput, calls=%fused_computation.86 | convolution fusion | flops 19333644288 | bytes 42467328 | tf_op jit(solution)/shard_map/dot_general | solution.py:41
  521.7 0.0 copy-done.3
  521.7 0.0 copy-start.6
  521.7 25.5 %bitcast_convert_fusion.5 = f32[1,768,3072]{1,2,0:T(8,128)} fusion(bf16[4096,768]{1,0:T(8,128)(2,1)S(1)} %copy-done.3, bf16[4096,3072]{1,0:T(8,128)(2,1)} %fusion.9), kind=kOutput, calls=%fused_computation.101 | convolution fusion | flops 19332071424 | bytes 40894464 | tf_op jit(solution)/shard_map/dot_general | solution.py:39
  547.1 0.0 copy-done.6
  547.2 31.9 %bitcast_convert_fusion.2 = f32[1,3072,768]{2,1,0:T(8,128)} fusion(bf16[4096,768]{1,0:T(8,128)(2,1)S(1)} %copy-done.6, bf16[4096,3072]{1,0:T(8,128)(2,1)} %convolution_convert_fusion.2), kind=kOutput, calls=%fused_computation.98 | convolution fusion | flops 19457900544 | bytes 40894464 | tf_op jit(solution)/shard_map/dot_general | solution.py:36
  579.1 56.6 %fusion.12 = bf16[4096,3072]{1,0:T(8,128)(2,1)} fusion(bf16[4096,3072]{1,0:T(8,128)(2,1)} %convolution_convert_fusion.2, bf16[4096,768]{1,0:T(8,128)(2,1)S(1)} %copy-done.6, bf16[4,3072,768]{2,1,0:T(8,128)(2,1)} %param.7), kind=kOutput, calls=%fused_computation.36 | convolution fusion | flops 19616759808 | bytes 61341696 | tf_op jit(solution)/shard_map/dot_general | solution.py:37
  635.6 0.0 copy-start.2
  635.6 27.4 %fusion.50 = bf16[4096,768]{1,0:T(8,128)(2,1)} fusion(bf16[4096,768]{1,0:T(8,128)(2,1)} %fusion.49, bf16[4096,3072]{1,0:T(8,128)(2,1)} %fusion.12, bf16[4,768,3072]{2,1,0:T(8,128)(2,1)} %param.6), kind=kOutput, calls=%fused_computation.87 | convolution fusion | flops 19333644288 | bytes 42467328 | tf_op jit(solution)/shard_map/dot_general | solution.py:41
  663.0 0.0 copy-done.2
  663.0 0.0 slice-start.4
  663.0 25.4 %bitcast_convert_fusion.6 = f32[1,768,3072]{1,2,0:T(8,128)} fusion(bf16[4096,768]{1,0:T(8,128)(2,1)S(1)} %copy-done.2, bf16[4096,3072]{1,0:T(8,128)(2,1)} %fusion.12), kind=kOutput, calls=%fused_computation.102 | convolution fusion | flops 19332071424 | bytes 40894464 | tf_op jit(solution)/shard_map/dot_general | solution.py:39
  688.5 0.0 slice-start.5
  688.5 0.0 slice-start.2
  688.5 34.7 %bitcast_convert_fusion.3 = f32[1,3072,768]{2,1,0:T(8,128)} fusion(bf16[4096,768]{1,0:T(8,128)(2,1)} %fusion.50, bf16[4096,3072]{1,0:T(8,128)(2,1)} %convolution_convert_fusion.3), kind=kOutput, calls=%fused_computation.99 | convolution fusion | flops 19457900544 | bytes 40894464 | tf_op jit(solution)/shard_map/dot_general | solution.py:36
  723.2 0.0 slice-done.4
  723.2 0.0 slice-done.5
  723.2 0.0 slice-start.3
  723.2 56.2 %fusion.142 = bf16[4096,3072]{1,0:T(8,128)(2,1)} fusion(bf16[4096,3072]{1,0:T(8,128)(2,1)} %convolution_convert_fusion.3, bf16[4096,768]{1,0:T(8,128)(2,1)S(1)} %bitcast.109, bf16[4,3072,768]{2,1,0:T(8,128)(2,1)} %param.7), kind=kOutput, calls=%fused_computation.39.clone.clone.clone.clone.clone.clone.1 | convolution fusion | flops 19616759808 | bytes 61341696 | tf_op jit(solution)/shard_map/dot_general | solution.py:37
  779.5 0.0 slice-done.2
  779.5 0.0 slice-done.3
  779.5 25.6 %convert_bitcast_fusion = f32[1,768,3072]{1,2,0:T(8,128)} fusion(bf16[4096,768]{1,0:T(8,128)(2,1)S(1)} %bitcast.107, bf16[4096,3072]{1,0:T(8,128)(2,1)} %fusion.142), kind=kOutput, calls=%fused_computation.81 | convolution fusion | flops 19332071424 | bytes 40894464 | tf_op jit(solution)/shard_map/dot_general | solution.py:39
  805.1 0.0 all-reduce.3.cloned.1.call-update
  805.1 656.7 %all-reduce.3.cloned.1.call-done = (f32[1,768,3072]{1,2,0:T(8,128)}, f32[1,768,3072]{1,2,0:T(8,128)}, f32[1,768,3072]{1,2,0:T(8,128)}, f32[1,768,3072]{1,2,0:T(8...) async-done(((f32[1,768,3072]{1,2,0:T(8,128)}, f32[1,768,3072]{1,2,0:T(8,128)}, ...) | async-done | bytes 75497488 | tf_op jit(solution)/shard_map/psum | solution.py:43
  1461.8 27.3 %pad_maximum_fusion = f32[4,768,3072]{1,2,0:T(8,128)} fusion(f32[1,768,3072]{1,2,0:T(8,128)} %get-tuple-element.4, f32[1,768,3072]{1,2,0:T(8,128)} %get-tuple-element.5, f32[1,768,3072]{1,2,0:T(8,128)} %get-tuple-element.6, f32[1,768,3072]{1,2,0:T(8,128)} %get-tuple-element.7), kind=kLoop, calls=%fused_computation.68 | loop fusion | flops 28311552 | bytes 75497472 | tf_op jit(solution)/shard_map/stack | solution.py:46
  1489.1 36.8 %copy.9 = f32[4,768,3072]{2,1,0:T(8,128)} copy(f32[4,768,3072]{1,2,0:T(8,128)} %pad_maximum_fusion) | data formatting | bytes 75497472
  1525.9 27.3 %pad_maximum_fusion.1 = f32[4,3072,768]{2,1,0:T(8,128)} fusion(f32[1,3072,768]{2,1,0:T(8,128)} %get-tuple-element.8, f32[1,3072,768]{2,1,0:T(8,128)} %get-tuple-element.9, f32[1,3072,768]{2,1,0:T(8,128)} %get-tuple-element.10, f32[1,3072,768]{2,1,0:T(8,128)} %get-tuple-element.11), kind=kLoop, calls=%fused_computation.69 | loop fusion | flops 28311552 | bytes 75497472 | tf_op jit(solution)/shard_map/stack | solution.py:46
  (3 shorter events, 0.0 us)
Async XLA Ops:
  7.2 1454.7 %all-reduce.3.cloned.1.call-start = ((), (), s32[]{:S(2)}) async-start(), calls=%async_computation | async-start | bytes 150994944 | tf_op jit(solution)/shard_map/psum | solution.py:43
  7.2 27.0 %copy-start = (bf16[4096,768]{1,0:T(8,128)(2,1)S(1)}, bf16[4096,768]{1,0:T(8,128)(2,1)}, u32[]{:S(2)}) copy-start(bf16[4096,768]{1,0:T(8,128)(2,1)} %param.4) | copy-start | bytes 18874372
  70.8 27.8 %copy-start.1 = (bf16[4096,768]{1,0:T(8,128)(2,1)S(1)}, bf16[4096,768]{1,0:T(8,128)(2,1)}, u32[]{:S(2)}) copy-start(bf16[4096,768]{1,0:T(8,128)(2,1)} %add_convert_fusion.3) | copy-start | bytes 18874372
  135.0 91.3 %slice-start = ((s8[6291456]{0:T(1024)(128)(4,1)}), s8[4194304]{0:T(1024)(128)(4,1)S(1)}, s32[]{:S(2)}) async-start(s8[6291456]{0:T(1024)(128)(4,1)} %bitcast.104), calls=%async_computation.1 | async-start | bytes 8388608
  162.1 64.1 %slice-start.1 = ((s8[6291456]{0:T(1024)(128)(4,1)}), s8[2097152]{0:T(1024)(128)(4,1)S(1)}, s32[]{:S(2)}) async-start(s8[6291456]{0:T(1024)(128)(4,1)} %bitcast.104), calls=%async_computation.2 | async-start | bytes 4194304
  263.1 33.7 %copy-start.7 = (bf16[4096,768]{1,0:T(8,128)(2,1)}, bf16[4096,768]{1,0:T(8,128)(2,1)S(1)}, u32[]{:S(2)}) copy-start(bf16[4096,768]{1,0:T(8,128)(2,1)S(1)} %multiply_convert_fusion) | copy-start | bytes 18874372
  352.7 27.5 %copy-start.4 = (bf16[4096,768]{1,0:T(8,128)(2,1)S(1)}, bf16[4096,768]{1,0:T(8,128)(2,1)}, u32[]{:S(2)}) copy-start(bf16[4096,768]{1,0:T(8,128)(2,1)} %add_convert_fusion.1) | copy-start | bytes 18874372
  380.2 25.4 %copy-start.5 = (bf16[4096,768]{1,0:T(8,128)(2,1)S(1)}, bf16[4096,768]{1,0:T(8,128)(2,1)}, u32[]{:S(2)}) copy-start(bf16[4096,768]{1,0:T(8,128)(2,1)} %fusion.48) | copy-start | bytes 18874372
  494.2 27.5 %copy-start.3 = (bf16[4096,768]{1,0:T(8,128)(2,1)S(1)}, bf16[4096,768]{1,0:T(8,128)(2,1)}, u32[]{:S(2)}) copy-start(bf16[4096,768]{1,0:T(8,128)(2,1)} %add_convert_fusion.2) | copy-start | bytes 18874372
  521.7 25.5 %copy-start.6 = (bf16[4096,768]{1,0:T(8,128)(2,1)S(1)}, bf16[4096,768]{1,0:T(8,128)(2,1)}, u32[]{:S(2)}) copy-start(bf16[4096,768]{1,0:T(8,128)(2,1)} %fusion.49) | copy-start | bytes 18874372
  635.6 27.4 %copy-start.2 = (bf16[4096,768]{1,0:T(8,128)(2,1)S(1)}, bf16[4096,768]{1,0:T(8,128)(2,1)}, u32[]{:S(2)}) copy-start(bf16[4096,768]{1,0:T(8,128)(2,1)} %add_convert_fusion.3) | copy-start | bytes 18874372
  663.0 60.1 %slice-start.4 = ((s8[6291456]{0:T(1024)(128)(4,1)}), s8[2097152]{0:T(1024)(128)(4,1)S(1)}, s32[]{:S(2)}) async-start(s8[6291456]{0:T(1024)(128)(4,1)} %bitcast.108), calls=%async_computation.5 | async-start | bytes 4194304
  688.5 34.7 %slice-start.5 = ((s8[6291456]{0:T(1024)(128)(4,1)}), s8[4194304]{0:T(1024)(128)(4,1)S(1)}, s32[]{:S(2)}) async-start(s8[6291456]{0:T(1024)(128)(4,1)} %bitcast.108), calls=%async_computation.6 | async-start | bytes 8388608
  688.5 91.0 %slice-start.2 = ((s8[6291456]{0:T(1024)(128)(4,1)}), s8[4194304]{0:T(1024)(128)(4,1)S(1)}, s32[]{:S(2)}) async-start(s8[6291456]{0:T(1024)(128)(4,1)} %bitcast.106), calls=%async_computation.3 | async-start | bytes 8388608
  723.2 56.3 %slice-start.3 = ((s8[6291456]{0:T(1024)(128)(4,1)}), s8[2097152]{0:T(1024)(128)(4,1)S(1)}, s32[]{:S(2)}) async-start(s8[6291456]{0:T(1024)(128)(4,1)} %bitcast.106), calls=%async_computation.4 | async-start | bytes 4194304
Sparse Core Ops, SparseCore 0:
  805.2 656.5 all-reduce.2
where the time goes:
time: 1570 us; the launch traced here: 1560 us
  matrix products  798 us (51%)
  waiting for transfers between devices  657 us (42%)
  other arithmetic  54.5 us (3%)
  local copies, waits for them, and re-layouts  36.8 us (2%)
    psum x1, waiting for transfers between devices, device_step(): lax.psum((local_in.astype(jnp.float32), local_out.astype(jnp.float32)), a...  657 us
    dot_general x4, matrix products, device_step(): lax.dot_general(grad_h, w_second_all[layer_idx], CONTRACT_COLS, preferred...  225 us
    dot_general x4, matrix products, device_step(): jnp.dot(activ, w_second_all[layer_idx], preferred_element_type=jnp.float32)  147 us
    dot_general x4, matrix products, device_step(): lax.dot_general(activ, grad_h, CONTRACT_ROWS, preferred_element_type=jnp....  133 us
    dot_general x4, matrix products, device_step(): jnp.dot(hidden, w_first_all[layer_idx], preferred_element_type=jnp.float32)  109 us
    dot_general x4, matrix products, device_step(): lax.dot_general(layer_in, grad_pre, CONTRACT_ROWS, preferred_element_type...  102 us
    dot_general x3, matrix products, device_step(): lax.dot_general(grad_pre, w_first_all[layer_idx], CONTRACT_COLS, preferre...  82.4 us
    another operation x2, other arithmetic, device_step(): return (jnp.stack(summed_in[::-1]), jnp.stack(summed_out[::-1]))  54.5 us
  transfers between devices with their start and end apart: 1, of which 1 were waited for; matrix products, arithmetic and copies ran while one was open for 0% of the time, Pallas kernels for 0%

commit v1 on v0

v1 whole, which is shorter than its diff:
```python
import functools
import math
import jax
import jax.numpy as jnp
from jax import lax
from jax.experimental import pallas as pl
from jax.experimental.pallas import tpu as pltpu
from jax.sharding import PartitionSpec as P

MESH = pl.DeviceIdType.MESH
ROWS_BOTH = (((0,), (0,)), ((), ()))
COLS_BOTH = (((1,), (1,)), ((), ()))
F32 = jnp.float32
BF16 = jnp.bfloat16

GELU_C = math.sqrt(2.0 / math.pi)
GELU_CK = GELU_C * 0.044715

HC = 512
BLK = 256
MT = 512
NS = 3
NF = 5
DELAY = 2


def backward_kernel(axis, layers, *refs):
    (gh_hbm, *rest) = refs
    h_hbm, rest = rest[:layers], rest[layers:]
    u_hbm, rest = rest[:layers], rest[layers:]
    (win_hbm, wout_hbm, gin_hbm, gout_hbm,
     gh, hb, back, ub, wi, wo, acc_out, acc_in, grads, pair, sums, full, recv0, recv1, recv2,
     gh_sem, h_sem, u_sem, wi_sem, wo_sem,
     pair_send, pair_recv, rs_send, rs_recv, ag_send, ag_recv, fin_local, fin_send, fin_recv) = rest
    recvs = (recv0, recv1, recv2)
    tokens, width = gh.shape
    per_layer = win_hbm.shape[2] // HC
    chunks = layers * per_layer
    pieces = 2 * chunks

    me = lax.axis_index(axis)
    core = lax.rem(me, 2)
    bit = [lax.rem(me // (2 << d), 2) for d in range(3)]
    peer = [me + (1 - 2 * bit[d]) * (2 << d) for d in range(3)]
    mate = me + 1 - 2 * core

    barrier = pltpu.get_barrier_semaphore()
    for other in (mate, *peer):
        pl.semaphore_signal(barrier, inc=1, device_id=(other,), device_id_type=MESH)
    pl.semaphore_wait(barrier, 4)

    def axis_of(p, k):
        return (p + k) % 3

    def kept(p, k):
        off = 0
        for j in range(k + 1):
            off = off + bit[axis_of(p, j)] * (BLK >> (j + 1))
        return off

    def given(p, k):
        off = kept(p, k - 1) if k else 0
        return off + (1 - bit[axis_of(p, k)]) * (BLK >> (k + 1))

    def rows_at(off, size):
        return pl.ds(pl.multiple_of(off, 32), size)

    def pair_copy(n):
        return pltpu.make_async_remote_copy(
            src_ref=grads.at[lax.rem(n, 4), 1 - core], dst_ref=pair.at[lax.rem(n, 2)],
            send_sem=pair_send.at[lax.rem(n, 2)], recv_sem=pair_recv.at[lax.rem(n, 2)],
            device_id=(mate,), device_id_type=MESH)

    def rs_copy(n, k, p):
        size = BLK >> (k + 1)
        return pltpu.make_async_remote_copy(
            src_ref=sums.at[lax.rem(n, NS), p, rows_at(given(p, k), size)],
            dst_ref=recvs[k].at[lax.rem(n, 2), p],
            send_sem=rs_send.at[k, lax.rem(n, 2), p], recv_sem=rs_recv.at[k, lax.rem(n, 2), p],
            device_id=(peer[axis_of(p, k)],), device_id_type=MESH)

    def ag_copy(n, k, p):
        part = full.at[lax.rem(n, NF), p, rows_at(kept(p, k), BLK >> (k + 1))]
        return pltpu.make_async_remote_copy(
            src_ref=part, dst_ref=part,
            send_sem=ag_send.at[k, lax.rem(n, 2), p], recv_sem=ag_recv.at[k, lax.rem(n, 2), p],
            device_id=(peer[axis_of(p, k)],), device_id_type=MESH)

    def ag_wait(n, k, p):
        ag_copy(n, k, p).wait_send()
        part = full.at[lax.rem(n, NF), p, rows_at(given(p, k), BLK >> (k + 1))]
        pltpu.make_async_remote_copy(
            src_ref=part, dst_ref=part,
            send_sem=ag_send.at[k, lax.rem(n, 2), p], recv_sem=ag_recv.at[k, lax.rem(n, 2), p],
            device_id=(peer[axis_of(p, k)],), device_id_type=MESH).wait_recv()

    def fin_copies(n, p, is_in, owner):
        chunk = n // 2
        layer = layers - 1 - chunk // per_layer
        first = pl.multiple_of(lax.rem(chunk, per_layer) * HC + owner * BLK, BLK)
        if is_in:
            dst = gin_hbm.at[layer, pl.ds(p * BLK, BLK), pl.ds(first, BLK)]
        else:
            dst = gout_hbm.at[layer, pl.ds(first, BLK), pl.ds(p * BLK, BLK)]
        src = full.at[lax.rem(n, NF), p]
        slot = lax.rem(n, 2)

        def local():
            return pltpu.make_async_copy(src, dst, fin_local.at[slot, p])

        def remote():
            return pltpu.make_async_remote_copy(
                src_ref=src, dst_ref=dst, send_sem=fin_send.at[slot, p], recv_sem=fin_recv.at[slot, p],
                device_id=(mate,), device_id_type=MESH)
        return local, remote

    def stage(n, body):
        pl.when(jnp.logical_and(n >= 0, n < pieces))(lambda: body(n))

    def both_kinds(n, body):
        pl.when(lax.rem(n, 2) == 0)(lambda: body(False))
        pl.when(lax.rem(n, 2) == 1)(lambda: body(True))

    def add_received(n, k):
        for p in range(3):
            rs_copy(n, k, p).wait()
        for p in range(3):
            rows = rows_at(kept(p, k), BLK >> (k + 1))
            total = sums[lax.rem(n, NS), p, rows] + recvs[k][lax.rem(n, 2), p]
            if k == 2:
                full[lax.rem(n, NF), p, rows] = total
            else:
                sums[lax.rem(n, NS), p, rows] = total

    def halve_last(n):
        add_received(n, 2)

    def halve(k, n):
        add_received(n, k)
        for p in range(3):
            rs_copy(n, k + 1, p).start()

    def add_pair(n):
        pair_copy(n).wait()
        for p in range(3):
            sums[lax.rem(n, NS), p] = (grads[lax.rem(n, 4), core, p].astype(F32)
                                       + pair[lax.rem(n, 2), p].astype(F32))
        for p in range(3):
            rs_copy(n, 0, p).start()

    def halving_side(t):
        stage(t - DELAY - 4, halve_last)
        stage(t - DELAY - 3, functools.partial(halve, 1))
        stage(t - DELAY - 2, functools.partial(halve, 0))
        stage(t - DELAY - 1, add_pair)
        stage(t - DELAY, lambda n: pair_copy(n).start())

    def finish_wait(n):
        def body(is_in):
            for p in range(3):
                local, remote = fin_copies(n, p, is_in, core)
                local().wait()
                remote().wait_send()
                fin_copies(n, p, is_in, 1 - core)[1]().wait_recv()
        both_kinds(n, body)

    def finish_start(n):
        for p in range(3):
            ag_wait(n, 0, p)

        def body(is_in):
            for p in range(3):
                local, remote = fin_copies(n, p, is_in, core)
                remote().start()
                local().start()
        both_kinds(n, body)

    def double(k, n):
        for p in range(3):
            ag_wait(n, k + 1, p)
        for p in range(3):
            ag_copy(n, k, p).start()

    def double_first(n):
        for p in range(3):
            ag_copy(n, 2, p).start()

    def doubling_side(t):
        stage(t - DELAY - 8, finish_wait)
        stage(t - DELAY - 7, finish_start)
        stage(t - DELAY - 6, functools.partial(double, 0))
        stage(t - DELAY - 5, functools.partial(double, 1))
        stage(t - DELAY - 4, double_first)

    def chunk_copies(i, layer_refs):
        layer = layers - 1 - i // per_layer
        cols = pl.ds(pl.multiple_of(lax.rem(i, per_layer) * HC, HC), HC)
        slot = lax.rem(i, 2)
        return (pltpu.make_async_copy(layer_refs.at[:, cols], ub.at[slot], u_sem.at[slot]),
                pltpu.make_async_copy(win_hbm.at[layer, :, cols], wi.at[slot], wi_sem.at[slot]),
                pltpu.make_async_copy(wout_hbm.at[layer, cols, :], wo.at[slot], wo_sem.at[slot]))

    def start_chunk(i):
        for k in range(layers):
            @pl.when(layers - 1 - i // per_layer == k)
            def _():
                for copy in chunk_copies(i, u_hbm[k]):
                    copy.start()

    def start_hidden(j):
        for k in range(layers):
            @pl.when(layers - 1 - j == k)
            def _():
                pltpu.make_async_copy(h_hbm[k], hb.at[lax.rem(j, 2)], h_sem.at[lax.rem(j, 2)]).start()

    def tile(m, slot, hslot):
        rows = pl.ds(pl.multiple_of(m * MT, MT), MT)
        u = ub[slot, rows, :].astype(F32)
        u2 = u * u
        t = jnp.tanh(u * (GELU_C + GELU_CK * u2))
        cdf = 0.5 + 0.5 * t
        act = (u * cdf).astype(BF16)
        slope = cdf + (u * (1.0 - t * t)) * (0.5 * GELU_C + 1.5 * GELU_CK * u2)
        g = gh[rows, :]
        g_act = lax.dot_general(g, wo[slot], COLS_BOTH, preferred_element_type=F32).astype(BF16)
        acc_out[...] += lax.dot_general(act, g, ROWS_BOTH, preferred_element_type=F32)
        g_pre = (g_act.astype(F32) * slope).astype(BF16)
        acc_in[...] += lax.dot_general(hb[hslot, rows, :], g_pre, ROWS_BOTH, preferred_element_type=F32)
        back[rows, :] += lax.dot_general(g_pre, wi[slot], COLS_BOTH, preferred_element_type=F32)

    first_gh = pltpu.make_async_copy(gh_hbm, gh, gh_sem.at[0])
    first_gh.start()
    start_chunk(0)
    start_hidden(0)
    first_gh.wait()

    def chunk_step(i, carry):
        slot = lax.rem(i, 2)
        j = i // per_layer
        hslot = lax.rem(j, 2)

        @pl.when(i + 1 < chunks)
        def _():
            start_chunk(i + 1)

        @pl.when(lax.rem(i, per_layer) == 0)
        def _():
            pltpu.make_async_copy(h_hbm[0], hb.at[hslot], h_sem.at[hslot]).wait()

            @pl.when(j + 1 < layers)
            def _():
                start_hidden(j + 1)

            @pl.loop(0, tokens // MT)
            def _(m):
                back[pl.ds(pl.multiple_of(m * MT, MT), MT), :] = jnp.zeros((MT, width), F32)

        acc_out[...] = jnp.zeros_like(acc_out)
        acc_in[...] = jnp.zeros_like(acc_in)
        for copy in chunk_copies(i, u_hbm[0]):
            copy.wait()

        @pl.loop(0, 4)
        def _(q):
            t = 2 * i + q // 2
            pl.when(lax.rem(q, 2) == 0)(lambda: halving_side(t))
            pl.when(lax.rem(q, 2) == 1)(lambda: doubling_side(t))
            per_quarter = tokens // MT // 4

            @pl.loop(0, per_quarter)
            def _(m):
                tile(q * per_quarter + m, slot, hslot)

        n_out = lax.rem(2 * i, 4)
        for half in range(2):
            for p in range(3):
                grads[n_out, half, p] = acc_out[half * BLK:(half + 1) * BLK, p * BLK:(p + 1) * BLK].astype(BF16)
                grads[n_out + 1, half, p] = acc_in[p * BLK:(p + 1) * BLK, half * BLK:(half + 1) * BLK].astype(BF16)

        @pl.when(jnp.logical_and(lax.rem(i, per_layer) == per_layer - 1, i + 1 < chunks))
        def _():
            @pl.loop(0, tokens // MT)
            def _(m):
                rows = pl.ds(pl.multiple_of(m * MT, MT), MT)
                gh[rows, :] = gh[rows, :] + back[rows, :].astype(BF16)
        return carry

    lax.fori_loop(0, chunks, chunk_step, 0)

    def drain(t, carry):
        halving_side(t)
        doubling_side(t)
        return carry

    lax.fori_loop(pieces, pieces + DELAY + 8, drain, 0)


def copy_kernel(a_ref, b_ref, c_ref, d_ref):
    c_ref[...] = a_ref[...]
    d_ref[...] = b_ref[...]


def solution(mesh):
    axis = mesh.axis_names[0]

    def grad_program(tokens, targets, w_in, w_out):
        total_tokens, width = tokens.shape
        target_scale = 1.0 + 16.0 * math.sqrt(total_tokens / width)
        loss_coef = 1.0 / (target_scale * math.sqrt(total_tokens))
        layers, _, hidden_width = w_in.shape

        def device_step(tok_rows, tgt_rows, w_first, w_second):
            rows = tok_rows.shape[0]
            hidden = tok_rows
            saved_h, saved_u = [], []
            for layer in range(layers):
                pre = jnp.dot(hidden, w_first[layer], preferred_element_type=F32).astype(BF16)
                act = jax.nn.gelu(pre.astype(F32)).astype(BF16)
                saved_h.append(hidden)
                saved_u.append(pre)
                branch = jnp.dot(act, w_second[layer], preferred_element_type=F32)
                hidden = (hidden.astype(F32) + branch).astype(BF16)
            error = hidden.astype(F32) - tgt_rows.astype(F32)
            grad_h = (error * loss_coef).astype(BF16)

            any_spec = pl.BlockSpec(memory_space=pl.ANY)
            dma = pltpu.SemaphoreType.DMA
            flops = 8 * rows * width * hidden_width * layers
            summed_in, summed_out = pl.pallas_call(
                functools.partial(backward_kernel, axis, layers),
                out_shape=(jax.ShapeDtypeStruct(w_first.shape, F32), jax.ShapeDtypeStruct(w_second.shape, F32)),
                in_specs=[any_spec] * (3 + 2 * layers),
                out_specs=(any_spec, any_spec),
                scratch_shapes=[
                    pltpu.VMEM((rows, width), BF16),
                    pltpu.VMEM((2, rows, width), BF16),
                    pltpu.VMEM((rows, width), F32),
                    pltpu.VMEM((2, rows, HC), BF16),
                    pltpu.VMEM((2, width, HC), BF16),
                    pltpu.VMEM((2, HC, width), BF16),
                    pltpu.VMEM((HC, width), F32),
                    pltpu.VMEM((width, HC), F32),
                    pltpu.VMEM((4, 2, 3, BLK, BLK), BF16),
                    pltpu.VMEM((2, 3, BLK, BLK), BF16),
                    pltpu.VMEM((NS, 3, BLK, BLK), F32),
                    pltpu.VMEM((NF, 3, BLK, BLK), F32),
                    pltpu.VMEM((2, 3, BLK // 2, BLK), F32),
                    pltpu.VMEM((2, 3, BLK // 4, BLK), F32),
                    pltpu.VMEM((2, 3, BLK // 8, BLK), F32),
                    dma((1,)), dma((2,)), dma((2,)), dma((2,)), dma((2,)),
                    dma((2,)), dma((2,)),
                    dma((3, 2, 3)), dma((3, 2, 3)), dma((3, 2, 3)), dma((3, 2, 3)),
                    dma((2, 3)), dma((2, 3)), dma((2, 3)),
                ],
                compiler_params=pltpu.CompilerParams(
                    collective_id=0, has_side_effects=True, vmem_limit_bytes=67043328),
                cost_estimate=pl.CostEstimate(flops=flops, bytes_accessed=300 * 2**20, transcendentals=0),
                name="backward_allreduce",
            )(grad_h, *saved_h, *saved_u, w_first, w_second)

            steps = 3 * layers
            in_block = pl.BlockSpec((1, width // 3, hidden_width), lambda s: (s // 3, s % 3, 0))
            out_block = pl.BlockSpec((1, hidden_width // 3, width), lambda s: (s // 3, s % 3, 0))
            return pl.pallas_call(
                copy_kernel,
                grid=(steps,),
                out_shape=(jax.ShapeDtypeStruct(w_first.shape, F32), jax.ShapeDtypeStruct(w_second.shape, F32)),
                in_specs=[in_block, out_block],
                out_specs=(in_block, out_block),
                compiler_params=pltpu.CompilerParams(vmem_limit_bytes=60 * 2**20),
                name="copy_out",
            )(summed_in, summed_out)

        return jax.shard_map(device_step, mesh=mesh, in_specs=(P(axis), P(axis), P(), P()), out_specs=(P(), P()), check_vma=False)(tokens, targets, w_in, w_out)

    return grad_program
```

time: 1570 us -> 856 us (0.55)
  waiting for transfers between devices: 657 us -> 0 us
  Pallas kernels: 0 us -> 593 us
  matrix products: 798 us -> 257 us
  other arithmetic: 54.5 us -> 0.01 us
  local copies, waits for them, and re-layouts: 36.8 us -> 0.02 us
    psum x1 -> x0, waiting for transfers between devices: 657 us -> none  [device_step(): lax.psum((local_in.astype(jnp.float32), local_out.astype(jnp.float32)), a...]
    pallas_call x0 -> x2, Pallas kernels: none -> 593 us  [the longest x1 545 us: device_step(): pl.pallas_call(functools.partial(backward_kernel, axis, layers), out_shap...]
    dot_general x23 -> x8, matrix products: 798 us -> 257 us  [the longest x4 148 us: device_step(): branch = jnp.dot(act, w_second[layer], preferred_element_type=F32)]
    another operation x2 -> x0, other arithmetic: 54.5 us -> none  [device_step(): return (jnp.stack(summed_in[::-1]), jnp.stack(summed_out[::-1]))]
    unnamed x29 -> x8, local copies, waits for them, and re-layouts: 36.8 us -> 0.02 us
  transfers between devices with their start and end apart: 1 -> 0, of which waited for: 1 -> 0; matrix products, arithmetic and copies ran while one was open for 0% -> 0% of each run, Pallas kernels for 0% -> 0%
where the time goes in v1:
time: 856 us; the launch traced here: 851 us
  Pallas kernels  593 us (69%)
  matrix products  257 us (30%)
    pallas_call x1, Pallas kernels, device_step(): pl.pallas_call(functools.partial(backward_kernel, axis, layers), out_shap...  545 us
    dot_general x4, matrix products, device_step(): branch = jnp.dot(act, w_second[layer], preferred_element_type=F32)  148 us
    dot_general x4, matrix products, device_step(): jnp.dot(hidden, w_first[layer], preferred_element_type=F32).astype(BF16)  109 us
    pallas_call x1, Pallas kernels, device_step(): pl.pallas_call(copy_kernel, grid=(steps,), out_shape=(jax.ShapeDtypeStruc...  48.3 us

profile of v1, /device:TPU:0, one launch (start us, length us, event | category | flops | bytes accessed | tf_op | source)
XLA Modules:
  0.0 850.7 jit_solution(5557300273784211297)
XLA Ops:
  0.6 0.0 copy-start
  0.6 27.0 %convolution_convert_fusion.3.refs_5_ = bf16[4096,3072]{1,0:T(8,128)(2,1)} fusion(bf16[4096,768]{1,0:T(8,128)(2,1)} %refs_1_.1, bf16[4,768,3072]{2,1,0:T(8,128)(2,1)} %refs_9_.1), kind=kOutput, calls=%fused_computation.47 | convolution fusion | flops 19339935744 | bytes 36175872 | tf_op jit(solution)/shard_map/dot_general | solution.py:317
  27.7 0.0 copy-done
  27.7 36.4 %add_convert_fusion.3.refs_2_ = bf16[4096,768]{1,0:T(8,128)(2,1)} fusion(bf16[4096,768]{1,0:T(8,128)(2,1)S(1)} %copy-done, bf16[4096,3072]{1,0:T(8,128)(2,1)} %convolution_convert_fusion.3.refs_5_, bf16[4,3072,768]{2,1,0:T(8,128)(2,1)} %refs_10_.1), kind=kOutput, calls=%fused_computation.52 | convolution fusion | flops 19462619136 | bytes 42467328 | tf_op jit(solution)/shard_map/dot_general | solution.py:321
  64.1 0.0 copy-start.1
  64.1 27.3 %convolution_convert_fusion.2.refs_6_ = bf16[4096,3072]{1,0:T(8,128)(2,1)} fusion(bf16[4096,768]{1,0:T(8,128)(2,1)} %add_convert_fusion.3.refs_2_, bf16[4,768,3072]{2,1,0:T(8,128)(2,1)} %refs_9_.1), kind=kOutput, calls=%fused_computation.46 | convolution fusion | flops 19339935744 | bytes 36175872 | tf_op jit(solution)/shard_map/dot_general | solution.py:317
  91.4 0.0 copy-done.1
  91.4 36.5 %add_convert_fusion.2.refs_3_ = bf16[4096,768]{1,0:T(8,128)(2,1)} fusion(bf16[4096,768]{1,0:T(8,128)(2,1)S(1)} %copy-done.1, bf16[4096,3072]{1,0:T(8,128)(2,1)} %convolution_convert_fusion.2.refs_6_, bf16[4,3072,768]{2,1,0:T(8,128)(2,1)} %refs_10_.1), kind=kOutput, calls=%fused_computation.51 | convolution fusion | flops 19462619136 | bytes 42467328 | tf_op jit(solution)/shard_map/dot_general | solution.py:321
  127.9 0.0 slice-start
  127.9 27.2 %convolution_convert_fusion.1.refs_7_ = bf16[4096,3072]{1,0:T(8,128)(2,1)} fusion(bf16[4096,768]{1,0:T(8,128)(2,1)} %add_convert_fusion.2.refs_3_, bf16[4,768,3072]{2,1,0:T(8,128)(2,1)} %refs_9_.1), kind=kOutput, calls=%fused_computation.45 | convolution fusion | flops 19339935744 | bytes 36175872 | tf_op jit(solution)/shard_map/dot_general | solution.py:317
  155.1 0.0 slice-start.1
  155.1 37.3 %add_convert_fusion.1.refs_4_ = bf16[4096,768]{1,0:T(8,128)(2,1)} fusion(bf16[4096,768]{1,0:T(8,128)(2,1)} %add_convert_fusion.2.refs_3_, bf16[4096,3072]{1,0:T(8,128)(2,1)} %convolution_convert_fusion.1.refs_7_, bf16[4,3072,768]{2,1,0:T(8,128)(2,1)} %refs_10_.1), kind=kOutput, calls=%fused_computation.50 | convolution fusion | flops 19462619136 | bytes 42467328 | tf_op jit(solution)/shard_map/dot_general | solution.py:321
  192.4 27.1 %convolution_convert_fusion.refs_8_ = bf16[4096,3072]{1,0:T(8,128)(2,1)} fusion(bf16[4096,768]{1,0:T(8,128)(2,1)} %add_convert_fusion.1.refs_4_, bf16[4,768,3072]{2,1,0:T(8,128)(2,1)} %refs_9_.1), kind=kOutput, calls=%fused_computation.44 | convolution fusion | flops 19339935744 | bytes 36175872 | tf_op jit(solution)/shard_map/dot_general | solution.py:317
  219.5 0.0 slice-done
  219.5 0.0 slice-done.1
  219.5 37.7 %multiply_convert_fusion.refs_0_ = bf16[4096,768]{1,0:T(8,128)(2,1)} fusion(bf16[4096,768]{1,0:T(8,128)(2,1)S(1)} %bitcast.29, bf16[4096,3072]{1,0:T(8,128)(2,1)} %convolution_convert_fusion.refs_8_, bf16[4096,768]{1,0:T(8,128)(2,1)} %add_convert_fusion.1.refs_4_, bf16[4,3072,768]{2,1,0:T(8,128)(2,1)} %refs_10_.1), kind=kOutput, calls=%fused_computation.48 | convolution fusion | flops 19478347776 | bytes 48758784 | tf_op jit(solution)/shard_map/dot_general | solution.py:321
  257.2 545.0 %backward_allreduce.1 = (f32[4,768,3072]{2,1,0:T(8,128)}, f32[4,3072,768]{2,1,0:T(8,128)}) custom-call(bf16[4096,768]{1,0:T(8,128)(2,1)} %multiply_convert_fusion.refs_0_, bf16[4096,768]{1,0:T(8,128)(2,1)} %refs_1_.1, bf16[4096,768]{1,0:T(8,128)(2,1)} %add_convert_fusion.3.refs_2_, bf16[4096,768]{1,0:T(8,128)(2,1)} %add_convert_fusion.2.refs_3_, ...), custom_call_target="tpu_custom_call" | custom-call | flops 309237645312 | bytes 314572800 | tf_op jit(solution)/shard_map/backward_allreduce/pallas_call | solution.py:329
  802.2 48.3 %copy_out.1 = (f32[4,768,3072]{2,1,0:T(8,128)}, f32[4,3072,768]{2,1,0:T(8,128)}) custom-call(f32[4,768,3072]{2,1,0:T(8,128)} %get-tuple-element.4.a_ref, f32[4,3072,768]{2,1,0:T(8,128)} %get-tuple-element.5.b_ref), custom_call_target="tpu_custom_call" | custom-call | tf_op jit(solution)/shard_map/copy_out/pallas_call | solution.py:364
  (1 shorter events, 0.0 us)
Async XLA Ops:
  0.6 27.0 %copy-start = (bf16[4096,768]{1,0:T(8,128)(2,1)S(1)}, bf16[4096,768]{1,0:T(8,128)(2,1)}, u32[]{:S(2)}) copy-start(bf16[4096,768]{1,0:T(8,128)(2,1)} %refs_1_.1) | copy-start | bytes 18874372
  64.1 27.3 %copy-start.1 = (bf16[4096,768]{1,0:T(8,128)(2,1)S(1)}, bf16[4096,768]{1,0:T(8,128)(2,1)}, u32[]{:S(2)}) copy-start(bf16[4096,768]{1,0:T(8,128)(2,1)} %add_convert_fusion.3.refs_2_) | copy-start | bytes 18874372
  127.9 91.6 %slice-start = ((s8[6291456]{0:T(1024)(128)(4,1)}), s8[4194304]{0:T(1024)(128)(4,1)S(1)}, s32[]{:S(2)}) async-start(s8[6291456]{0:T(1024)(128)(4,1)} %bitcast.28), calls=%async_computation | async-start | bytes 8388608
  155.1 64.4 %slice-start.1 = ((s8[6291456]{0:T(1024)(128)(4,1)}), s8[2097152]{0:T(1024)(128)(4,1)S(1)}, s32[]{:S(2)}) async-start(s8[6291456]{0:T(1024)(128)(4,1)} %bitcast.28), calls=%async_computation.1 | async-start | bytes 4194304

commit v2 on v1

--- a/solution.py
+++ b/solution.py
@@ -21,6 +21,8 @@
 MT = 512
 NS = 3
 NF = 5
+FC = 3072
+FT = 512
 DELAY = 2
 
 
@@ -295,6 +297,105 @@
     lax.fori_loop(pieces, pieces + DELAY + 8, drain, 0)
 
 
+def forward_kernel(layers, coef, *refs):
+    (x_hbm, t_hbm, win_hbm, wout_hbm), rest = refs[:4], refs[4:]
+    gh_hbm, rest = rest[0], rest[1:]
+    h_hbm, rest = rest[:layers - 1], rest[layers - 1:]
+    u_hbm, rest = rest[:layers], rest[layers:]
+    win, wout, hid, branch, ubuf, hbuf, tbuf, gbuf, w_sem, x_sem, t_sem, u_sem, h_sem, g_sem = rest
+    tokens = x_hbm.shape[0]
+    chunks = win.shape[2] // FC
+    tiles = tokens // FT
+
+    def weight_copies(k):
+        return (pltpu.make_async_copy(win_hbm.at[k], win.at[k], w_sem.at[k, 0]),
+                pltpu.make_async_copy(wout_hbm.at[k], wout.at[k], w_sem.at[k, 1]))
+
+    def tile_rows(r):
+        return pl.ds(pl.multiple_of(r * FT, FT), FT)
+
+    def load_x(r):
+        return pltpu.make_async_copy(x_hbm.at[tile_rows(r)], hid.at[lax.rem(r, 2)], x_sem.at[lax.rem(r, 2)])
+
+    def load_t(r):
+        return pltpu.make_async_copy(t_hbm.at[tile_rows(r)], tbuf, t_sem.at[0])
+
+    def step_of(r, k, c):
+        return (r * layers + k) * chunks + c
+
+    def store_u(r, k, c):
+        cols = pl.ds(pl.multiple_of(c * FC, FC), FC)
+        slot = lax.rem(step_of(r, k, c), 2)
+        return pltpu.make_async_copy(ubuf.at[slot], u_hbm[k].at[tile_rows(r), cols], u_sem.at[slot])
+
+    def store_h(r, k):
+        return pltpu.make_async_copy(hbuf.at[k % 2], h_hbm[k].at[tile_rows(r)], h_sem.at[k % 2])
+
+    def store_g(r):
+        return pltpu.make_async_copy(gbuf, gh_hbm.at[tile_rows(r)], g_sem.at[0])
+
+    load_x(0).start()
+    for k in range(layers):
+        for copy in weight_copies(k):
+            copy.start()
+
+    @pl.loop(0, tiles)
+    def _(r):
+        cur = lax.rem(r, 2)
+        load_x(r).wait()
+        load_t(r).start()
+
+        @pl.when(r + 1 < tiles)
+        def _():
+            load_x(r + 1).start()
+
+        for k in range(layers):
+            @pl.when(r == 0)
+            def _():
+                for copy in weight_copies(k):
+                    copy.wait()
+
+            branch[...] = hid[cur].astype(F32)
+
+            @pl.loop(0, chunks)
+            def _(c):
+                @pl.when(step_of(r, k, c) >= 2)
+                def _():
+                    store_u(r, k, c).wait()
+                cols = pl.ds(pl.multiple_of(c * FC, FC), FC)
+                pre = jnp.dot(hid[cur], win[k, :, cols], preferred_element_type=F32).astype(BF16)
+                ubuf[lax.rem(step_of(r, k, c), 2)] = pre
+                u = pre.astype(F32)
+                t = jnp.tanh(u * (GELU_C + GELU_CK * (u * u)))
+                act = (u * (0.5 + 0.5 * t)).astype(BF16)
+                branch[...] += jnp.dot(act, wout[k, cols, :], preferred_element_type=F32)
+                store_u(r, k, c).start()
+
+            new = branch[...].astype(BF16)
+            if k < layers - 1:
+                @pl.when(r * layers + k >= 2)
+                def _():
+                    store_h(r, k).wait()
+                hid[cur] = new
+                hbuf[k % 2] = new
+                store_h(r, k).start()
+            else:
+                load_t(r).wait()
+
+                @pl.when(r > 0)
+                def _():
+                    store_g(r).wait()
+                gbuf[...] = ((new.astype(F32) - tbuf[...].astype(F32)) * coef).astype(BF16)
+                store_g(r).start()
+
+    for slot in range(2):
+        cols = pl.ds(0, FC)
+        pltpu.make_async_copy(ubuf.at[slot], u_hbm[0].at[pl.ds(0, FT), cols], u_sem.at[slot]).wait()
+    for k in range(min(2, layers - 1)):
+        store_h(tiles - 1, k).wait()
+    store_g(tiles - 1).wait()
+
+
 def copy_kernel(a_ref, b_ref, c_ref, d_ref):
     c_ref[...] = a_ref[...]
     d_ref[...] = b_ref[...]
@@ -311,20 +412,29 @@
 
         def device_step(tok_rows, tgt_rows, w_first, w_second):
             rows = tok_rows.shape[0]
-            hidden = tok_rows
-            saved_h, saved_u = [], []
-            for layer in range(layers):
-                pre = jnp.dot(hidden, w_first[layer], preferred_element_type=F32).astype(BF16)
-                act = jax.nn.gelu(pre.astype(F32)).astype(BF16)
-                saved_h.append(hidden)
-                saved_u.append(pre)
-                branch = jnp.dot(act, w_second[layer], preferred_element_type=F32)
-                hidden = (hidden.astype(F32) + branch).astype(BF16)
-            error = hidden.astype(F32) - tgt_rows.astype(F32)
-            grad_h = (error * loss_coef).astype(BF16)
-
             any_spec = pl.BlockSpec(memory_space=pl.ANY)
             dma = pltpu.SemaphoreType.DMA
+            row_shape = jax.ShapeDtypeStruct((rows, width), BF16)
+            pre_shape = jax.ShapeDtypeStruct((rows, hidden_width), BF16)
+            forward = pl.pallas_call(
+                functools.partial(forward_kernel, layers, loss_coef),
+                out_shape=[row_shape] * layers + [pre_shape] * layers,
+                in_specs=[any_spec] * 4,
+                out_specs=[any_spec] * (2 * layers),
+                scratch_shapes=[
+                    pltpu.VMEM(w_first.shape, BF16), pltpu.VMEM(w_second.shape, BF16),
+                    pltpu.VMEM((2, FT, width), BF16), pltpu.VMEM((FT, width), F32),
+                    pltpu.VMEM((2, FT, FC), BF16), pltpu.VMEM((2, FT, width), BF16),
+                    pltpu.VMEM((FT, width), BF16), pltpu.VMEM((FT, width), BF16),
+                    dma((layers, 2)), dma((2,)), dma((1,)), dma((2,)), dma((2,)), dma((1,)),
+                ],
+                compiler_params=pltpu.CompilerParams(vmem_limit_bytes=67043328),
+                cost_estimate=pl.CostEstimate(flops=4 * rows * width * hidden_width * layers,
+                                              bytes_accessed=200 * 2**20, transcendentals=0),
+                name="forward",
+            )(tok_rows, tgt_rows, w_first, w_second)
+            grad_h, saved_h, saved_u = forward[0], [tok_rows, *forward[1:layers]], forward[layers:]
+
             flops = 8 * rows * width * hidden_width * layers
             summed_in, summed_out = pl.pallas_call(
                 functools.partial(backward_kernel, axis, layers),

time: 856 us -> 784 us (0.916)
  matrix products: 257 us -> 0 us
  Pallas kernels: 593 us -> 783 us
    dot_general x8 -> x0, matrix products: 257 us -> none  [the longest x4 148 us: device_step(): branch = jnp.dot(act, w_second[layer], preferred_element_type=F32)]
    pallas_call x0 -> x1, Pallas kernels: none -> 190 us  [device_step(): pl.pallas_call(functools.partial(forward_kernel, layers, loss_coef), out_...]
where the time goes in v2:
time: 784 us
  Pallas kernels  783 us (100%)
    pallas_call x1, Pallas kernels, device_step(): pl.pallas_call(functools.partial(backward_kernel, axis, layers), out_shap...  545 us
    pallas_call x1, Pallas kernels, device_step(): pl.pallas_call(functools.partial(forward_kernel, layers, loss_coef), out_...  190 us
    pallas_call x1, Pallas kernels, device_step(): pl.pallas_call(copy_kernel, grid=(steps,), out_shape=(jax.ShapeDtypeStruc...  48.3 us

profile of v2, /device:TPU:0, one launch (start us, length us, event | category | flops | bytes accessed | tf_op | source)
XLA Modules:
  0.0 783.6 jit_solution(8978100306971259769)
XLA Ops:
  0.6 189.7 %forward.1 = (bf16[4096,768]{1,0:T(8,128)(2,1)}, bf16[4096,768]{1,0:T(8,128)(2,1)}, bf16[4096,768]{1,0:T(8,128)(2,1)}, bf16[4096,768]{1,0:T(8,128)(2,1)}, bf16[4...) custom-call(bf16[4096,768]{1,0:T(8,128)(2,1)} %refs_1_.3, ...), custom_call_target="tpu_custom_call" | custom-call | flops 154618822656 | bytes 209715200 | tf_op jit(solution)/shard_map/forward/pallas_call | solution.py:419
  190.3 545.0 %backward_allreduce.1 = (f32[4,768,3072]{2,1,0:T(8,128)}, f32[4,3072,768]{2,1,0:T(8,128)}) custom-call(bf16[4096,768]{1,0:T(8,128)(2,1)} %get-tuple-element.12.refs_0_, bf16[4096,768]{1,0:T(8,128)(2,1)} %refs_1_.3, bf16[4096,768]{1,0:T(8,128)(2,1)} %get-tuple-element.13.refs_2_, bf16[4096,768]{1,0:T(8,128)(2,1)} %get-tuple-element.14.refs_3_, ...), custom_call_target="tpu_custom_call" | custom-call | flops 309237645312 | bytes 314572800 | tf_op jit(solution)/shard_map/backward_allreduce/pallas_call | solution.py:439
  735.3 48.3 %copy_out.1 = (f32[4,768,3072]{2,1,0:T(8,128)}, f32[4,3072,768]{2,1,0:T(8,128)}) custom-call(f32[4,768,3072]{2,1,0:T(8,128)} %get-tuple-element.20.a_ref, f32[4,3072,768]{2,1,0:T(8,128)} %get-tuple-element.21.b_ref), custom_call_target="tpu_custom_call" | custom-call | tf_op jit(solution)/shard_map/copy_out/pallas_call | solution.py:474

commit v3 on v2

--- a/solution.py
+++ b/solution.py
@@ -18,7 +18,7 @@
 
 HC = 512
 BLK = 256
-MT = 512
+MT = 1024
 NS = 3
 NF = 5
 FC = 3072
@@ -31,8 +31,8 @@
     h_hbm, rest = rest[:layers], rest[layers:]
     u_hbm, rest = rest[:layers], rest[layers:]
     (win_hbm, wout_hbm, gin_hbm, gout_hbm,
-     gh, hb, back, ub, wi, wo, acc_out, acc_in, grads, pair, sums, full, recv0, recv1, recv2,
-     gh_sem, h_sem, u_sem, wi_sem, wo_sem,
+     gh, hb, back, ub, wi, wo, acc_out, acc_in, grads, pair, sums, away, full, recv0, recv1, recv2,
+     first_sem, h_sem, u_sem, wi_sem, wo_sem,
      pair_send, pair_recv, rs_send, rs_recv, ag_send, ag_recv, fin_local, fin_send, fin_recv) = rest
     recvs = (recv0, recv1, recv2)
     tokens, width = gh.shape
@@ -69,14 +69,15 @@
 
     def pair_copy(n):
         return pltpu.make_async_remote_copy(
-            src_ref=grads.at[lax.rem(n, 4), 1 - core], dst_ref=pair.at[lax.rem(n, 2)],
+            src_ref=grads.at[lax.rem(n, 3), 1 - core], dst_ref=pair.at[lax.rem(n, 2)],
             send_sem=pair_send.at[lax.rem(n, 2)], recv_sem=pair_recv.at[lax.rem(n, 2)],
             device_id=(mate,), device_id_type=MESH)
 
     def rs_copy(n, k, p):
         size = BLK >> (k + 1)
+        src = sums.at[lax.rem(n, NS), p, rows_at(given(p, k) - kept(p, 0), size)] if k else away.at[p]
         return pltpu.make_async_remote_copy(
-            src_ref=sums.at[lax.rem(n, NS), p, rows_at(given(p, k), size)],
+            src_ref=src,
             dst_ref=recvs[k].at[lax.rem(n, 2), p],
             send_sem=rs_send.at[k, lax.rem(n, 2), p], recv_sem=rs_recv.at[k, lax.rem(n, 2), p],
             device_id=(peer[axis_of(p, k)],), device_id_type=MESH)
@@ -127,10 +128,11 @@
         for p in range(3):
             rs_copy(n, k, p).wait()
         for p in range(3):
-            rows = rows_at(kept(p, k), BLK >> (k + 1))
+            size = BLK >> (k + 1)
+            rows = rows_at(kept(p, k) - kept(p, 0), size)
             total = sums[lax.rem(n, NS), p, rows] + recvs[k][lax.rem(n, 2), p]
             if k == 2:
-                full[lax.rem(n, NF), p, rows] = total
+                full[lax.rem(n, NF), p, rows_at(kept(p, k), size)] = total
             else:
                 sums[lax.rem(n, NS), p, rows] = total
 
@@ -145,8 +147,10 @@
     def add_pair(n):
         pair_copy(n).wait()
         for p in range(3):
-            sums[lax.rem(n, NS), p] = (grads[lax.rem(n, 4), core, p].astype(F32)
-                                       + pair[lax.rem(n, 2), p].astype(F32))
+            for rows, dst in ((kept(p, 0), sums.at[lax.rem(n, NS), p]), (given(p, 0), away.at[p])):
+                rows = pl.ds(pl.multiple_of(rows, BLK // 2), BLK // 2)
+                dst[...] = (grads[lax.rem(n, 3), core, p, rows].astype(F32)
+                            + pair[lax.rem(n, 2), p, rows].astype(F32))
         for p in range(3):
             rs_copy(n, 0, p).start()
 
@@ -194,20 +198,30 @@
         stage(t - DELAY - 5, functools.partial(double, 1))
         stage(t - DELAY - 4, double_first)
 
-    def chunk_copies(i, layer_refs):
+    def pre_of(i, layer_refs):
+        cols = pl.ds(pl.multiple_of(lax.rem(i, per_layer) * HC, HC), HC)
+        return pltpu.make_async_copy(layer_refs.at[:, cols], ub.at[lax.rem(i, 2)], u_sem.at[lax.rem(i, 2)])
+
+    def weights_of(i):
         layer = layers - 1 - i // per_layer
         cols = pl.ds(pl.multiple_of(lax.rem(i, per_layer) * HC, HC), HC)
         slot = lax.rem(i, 2)
-        return (pltpu.make_async_copy(layer_refs.at[:, cols], ub.at[slot], u_sem.at[slot]),
-                pltpu.make_async_copy(win_hbm.at[layer, :, cols], wi.at[slot], wi_sem.at[slot]),
+        return (pltpu.make_async_copy(win_hbm.at[layer, :, cols], wi.at[slot], wi_sem.at[slot]),
                 pltpu.make_async_copy(wout_hbm.at[layer, cols, :], wo.at[slot], wo_sem.at[slot]))
+
+    def slice_copies(m):
+        rows = pl.ds(pl.multiple_of(m * MT, MT), MT)
+        return (pltpu.make_async_copy(gh_hbm.at[rows], gh.at[rows], first_sem.at[0, m]),
+                pltpu.make_async_copy(u_hbm[layers - 1].at[rows, pl.ds(0, HC)], ub.at[0, rows], first_sem.at[1, m]),
+                pltpu.make_async_copy(h_hbm[layers - 1].at[rows], hb.at[0, rows], first_sem.at[2, m]))
 
     def start_chunk(i):
         for k in range(layers):
             @pl.when(layers - 1 - i // per_layer == k)
             def _():
-                for copy in chunk_copies(i, u_hbm[k]):
-                    copy.start()
+                pre_of(i, u_hbm[k]).start()
+        for copy in weights_of(i):
+            copy.start()
 
     def start_hidden(j):
         for k in range(layers):
@@ -215,7 +229,7 @@
             def _():
                 pltpu.make_async_copy(h_hbm[k], hb.at[lax.rem(j, 2)], h_sem.at[lax.rem(j, 2)]).start()
 
-    def tile(m, slot, hslot):
+    def tile(with_back, m, slot, hslot):
         rows = pl.ds(pl.multiple_of(m * MT, MT), MT)
         u = ub[slot, rows, :].astype(F32)
         u2 = u * u
@@ -228,13 +242,16 @@
         acc_out[...] += lax.dot_general(act, g, ROWS_BOTH, preferred_element_type=F32)
         g_pre = (g_act.astype(F32) * slope).astype(BF16)
         acc_in[...] += lax.dot_general(hb[hslot, rows, :], g_pre, ROWS_BOTH, preferred_element_type=F32)
-        back[rows, :] += lax.dot_general(g_pre, wi[slot], COLS_BOTH, preferred_element_type=F32)
-
-    first_gh = pltpu.make_async_copy(gh_hbm, gh, gh_sem.at[0])
-    first_gh.start()
-    start_chunk(0)
-    start_hidden(0)
-    first_gh.wait()
+        if with_back:
+            back[rows, :] += lax.dot_general(g_pre, wi[slot], COLS_BOTH, preferred_element_type=F32)
+
+    for copy in weights_of(0):
+        copy.start()
+
+    @pl.loop(0, tokens // MT)
+    def _(m):
+        for copy in slice_copies(m):
+            copy.start()
 
     def chunk_step(i, carry):
         slot = lax.rem(i, 2)
@@ -247,7 +264,9 @@
 
         @pl.when(lax.rem(i, per_layer) == 0)
         def _():
-            pltpu.make_async_copy(h_hbm[0], hb.at[hslot], h_sem.at[hslot]).wait()
+            @pl.when(j > 0)
+            def _():
+                pltpu.make_async_copy(h_hbm[0], hb.at[hslot], h_sem.at[hslot]).wait()
 
             @pl.when(j + 1 < layers)
             def _():
@@ -259,8 +278,12 @@
 
         acc_out[...] = jnp.zeros_like(acc_out)
         acc_in[...] = jnp.zeros_like(acc_in)
-        for copy in chunk_copies(i, u_hbm[0]):
+        for copy in weights_of(i):
             copy.wait()
+
+        @pl.when(i > 0)
+        def _():
+            pre_of(i, u_hbm[0]).wait()
 
         @pl.loop(0, 4)
         def _(q):
@@ -269,15 +292,26 @@
             pl.when(lax.rem(q, 2) == 1)(lambda: doubling_side(t))
             per_quarter = tokens // MT // 4
 
-            @pl.loop(0, per_quarter)
-            def _(m):
-                tile(q * per_quarter + m, slot, hslot)
-
-        n_out = lax.rem(2 * i, 4)
+            @pl.when(i == 0)
+            def _():
+                @pl.loop(0, per_quarter)
+                def _(m):
+                    for copy in slice_copies(q * per_quarter + m):
+                        copy.wait()
+
+            def tiles(with_back):
+                @pl.loop(0, per_quarter)
+                def _(m):
+                    tile(with_back, q * per_quarter + m, slot, hslot)
+
+            pl.when(j < layers - 1)(lambda: tiles(True))
+            pl.when(j == layers - 1)(lambda: tiles(False))
+
+        s_out, s_in = lax.rem(2 * i, 3), lax.rem(2 * i + 1, 3)
         for half in range(2):
             for p in range(3):
-                grads[n_out, half, p] = acc_out[half * BLK:(half + 1) * BLK, p * BLK:(p + 1) * BLK].astype(BF16)
-                grads[n_out + 1, half, p] = acc_in[p * BLK:(p + 1) * BLK, half * BLK:(half + 1) * BLK].astype(BF16)
+                grads[s_out, half, p] = acc_out[half * BLK:(half + 1) * BLK, p * BLK:(p + 1) * BLK].astype(BF16)
+                grads[s_in, half, p] = acc_in[p * BLK:(p + 1) * BLK, half * BLK:(half + 1) * BLK].astype(BF16)
 
         @pl.when(jnp.logical_and(lax.rem(i, per_layer) == per_layer - 1, i + 1 < chunks))
         def _():
@@ -450,14 +484,15 @@
                     pltpu.VMEM((2, HC, width), BF16),
                     pltpu.VMEM((HC, width), F32),
                     pltpu.VMEM((width, HC), F32),
-                    pltpu.VMEM((4, 2, 3, BLK, BLK), BF16),
+                    pltpu.VMEM((3, 2, 3, BLK, BLK), BF16),
                     pltpu.VMEM((2, 3, BLK, BLK), BF16),
-                    pltpu.VMEM((NS, 3, BLK, BLK), F32),
+                    pltpu.VMEM((NS, 3, BLK // 2, BLK), F32),
+                    pltpu.VMEM((3, BLK // 2, BLK), F32),
                     pltpu.VMEM((NF, 3, BLK, BLK), F32),
                     pltpu.VMEM((2, 3, BLK // 2, BLK), F32),
                     pltpu.VMEM((2, 3, BLK // 4, BLK), F32),
                     pltpu.VMEM((2, 3, BLK // 8, BLK), F32),
-                    dma((1,)), dma((2,)), dma((2,)), dma((2,)), dma((2,)),
+                    dma((3, rows // MT)), dma((2,)), dma((2,)), dma((2,)), dma((2,)),
                     dma((2,)), dma((2,)),
                     dma((3, 2, 3)), dma((3, 2, 3)), dma((3, 2, 3)), dma((3, 2, 3)),
                     dma((2, 3)), dma((2, 3)), dma((2, 3)),
@@ -468,9 +503,10 @@
                 name="backward_allreduce",
             )(grad_h, *saved_h, *saved_u, w_first, w_second)
 
-            steps = 3 * layers
-            in_block = pl.BlockSpec((1, width // 3, hidden_width), lambda s: (s // 3, s % 3, 0))
-            out_block = pl.BlockSpec((1, hidden_width // 3, width), lambda s: (s // 3, s % 3, 0))
+            cut = 6
+            steps = cut * layers
+            in_block = pl.BlockSpec((1, width // cut, hidden_width), lambda s: (s // cut, s % cut, 0))
+            out_block = pl.BlockSpec((1, hidden_width // cut, width), lambda s: (s // cut, s % cut, 0))
             return pl.pallas_call(
                 copy_kernel,
                 grid=(steps,),

time: 784 us -> 779 us (level)
    pallas_call x1, Pallas kernels: 545 us -> 534 us  [device_step(): pl.pallas_call(functools.partial(backward_kernel, axis, layers), out_shap...]
where the time goes in v3:
time: 779 us; the launch traced here: 778 us
  Pallas kernels  778 us (100%)
    pallas_call x1, Pallas kernels, device_step(): pl.pallas_call(functools.partial(backward_kernel, axis, layers), out_shap...  534 us
    pallas_call x1, Pallas kernels, device_step(): pl.pallas_call(functools.partial(forward_kernel, layers, loss_coef), out_...  190 us
    pallas_call x1, Pallas kernels, device_step(): pl.pallas_call(copy_kernel, grid=(steps,), out_shape=(jax.ShapeDtypeStruc...  54.1 us

profile of v3, /device:TPU:0, one launch (start us, length us, event | category | flops | bytes accessed | tf_op | source)
XLA Modules:
  0.0 778.5 jit_solution(1260663203563976841)
XLA Ops:
  0.6 189.7 %forward.1 = (bf16[4096,768]{1,0:T(8,128)(2,1)}, bf16[4096,768]{1,0:T(8,128)(2,1)}, bf16[4096,768]{1,0:T(8,128)(2,1)}, bf16[4096,768]{1,0:T(8,128)(2,1)}, bf16[4...) custom-call(bf16[4096,768]{1,0:T(8,128)(2,1)} %refs_1_.3, ...), custom_call_target="tpu_custom_call" | custom-call | flops 154618822656 | bytes 209715200 | tf_op jit(solution)/shard_map/forward/pallas_call | solution.py:453
  190.3 534.0 %backward_allreduce.1 = (f32[4,768,3072]{2,1,0:T(8,128)}, f32[4,3072,768]{2,1,0:T(8,128)}) custom-call(bf16[4096,768]{1,0:T(8,128)(2,1)} %get-tuple-element.12.refs_0_, bf16[4096,768]{1,0:T(8,128)(2,1)} %refs_1_.3, bf16[4096,768]{1,0:T(8,128)(2,1)} %get-tuple-element.13.refs_2_, bf16[4096,768]{1,0:T(8,128)(2,1)} %get-tuple-element.14.refs_3_, ...), custom_call_target="tpu_custom_call" | custom-call | flops 309237645312 | bytes 314572800 | tf_op jit(solution)/shard_map/backward_allreduce/pallas_call | solution.py:473
  724.4 54.1 %copy_out.1 = (f32[4,768,3072]{2,1,0:T(8,128)}, f32[4,3072,768]{2,1,0:T(8,128)}) custom-call(f32[4,768,3072]{2,1,0:T(8,128)} %get-tuple-element.20.a_ref, f32[4,3072,768]{2,1,0:T(8,128)} %get-tuple-element.21.b_ref), custom_call_target="tpu_custom_call" | custom-call | tf_op jit(solution)/shard_map/copy_out/pallas_call | solution.py:510
